TPU v7x, 32 devices: a whole 2x2x4 slice. The times are simulated.
32 devices in a mesh: gx: 8 (over z, x), gy: 4 (over y, core).
Axes of the slice: x: 2, y: 2, z: 4, core: 2. Of those that a mesh axis runs over, the one named last changes fastest.
Arguments:
- parcel_props: float32 [16, 131072], P(None, ('gx', 'gy')), may hold values from -6 to 6
- size_class: int32 [131072], P(('gx', 'gy')), may hold values from 0 to 7
- dest_owner: int32 [131072, 1], P(('gx', 'gy')), may hold values from 0 to 31; in each aligned block of 4096 rows (0 to 4095, 4096 to 8191, ...) at most 512 rows name the same one
- dest_local: int32 [131072], P(('gx', 'gy')), may hold values from 0 to 4095
- class_table: float32 [8, 16], replicated, may hold values from 0.5 to 2
- gas_density: float32 [256, 512], P('gx', 'gy'), may hold values from 0.5 to 2
- gas_rest: float32 [4, 256, 512], P(None, 'gx', 'gy'), may hold values from -6 to 6
Outputs:
- new_density: float32 [256, 512], P('gx', 'gy')
- new_rest: float32 [4, 256, 512], P(None, 'gx', 'gy')
Inputs may be any that keep to these rules, and one draw needn't show every extreme that they name: `dest_owner`: among the parcels of one device, no owner device is named by more than 512 of them, a bound that some block reaches.
All inputs are finite; a program needn't handle non-finite values.
Results may differ from a plain program's by a relative error of at most 0.00015.
Values sent between devices are 32-bit elements; how exact they have to be, the bound alone decides.
No kernel may reach another device: no remote copies, remote signals or barrier semaphores. Data moves between devices by JAX's collectives and lax.ppermute only.
A program may use at most 64 MiB of HBM per device.

v0:
```python
import math
import jax
import jax.numpy as jnp
from jax import lax
from jax.sharding import PartitionSpec as P


def with_halo(shard, sides, width):
    for axis, dim in sides:
        devices, length = (lax.axis_size(axis), shard.shape[dim])
        up = [(i, (i + 1) % devices) for i in range(devices - 1)]
        down = [(j, i) for i, j in up]
        last = lax.slice_in_dim(shard, length - width, length, axis=dim)
        leading = lax.slice_in_dim(shard, 0, width, axis=dim)
        before = lax.ppermute(last, axis, up)
        after = lax.ppermute(leading, axis, down)
        shard = jnp.concatenate([before, shard, after], axis=dim)
    return shard


def sources_of(props, classes, gas, table):
    count = table.shape[0]
    picks = (classes[None, :] == jnp.arange(count, dtype=jnp.int32)[:, None]).astype(jnp.float32)
    coef = jnp.dot(
        table.T, picks, precision=lax.Precision.HIGHEST, preferred_element_type=jnp.float32
    )
    mass = jnp.exp(0.5 * props[0])
    density = gas[0]
    velocity = gas[1:4] / density
    theta = gas[4] / density
    slip = props[1:4] - velocity
    rate = coef[0] * jax.nn.softplus(props[4] - theta)
    evapor = mass * (1.0 - jnp.exp(-rate))
    dragged = 1.0 - jnp.exp(-coef[1] * jnp.sqrt(1.0 + jnp.sum(slip * slip, axis=0)))
    moment = evapor * coef[2:5] * props[1:4] + mass * dragged * slip
    energy = evapor * (props[4] + jnp.sum(coef[5:] * props[5:], axis=0))
    return jnp.concatenate([evapor[None], moment, energy[None]], axis=0)


def cell_hot(cells, first, width):
    return (cells[None, :] == (first + jnp.arange(width, dtype=jnp.int32))[:, None]).astype(
        jnp.float32
    )


def look_up(table, cells):
    total = table.shape[1]
    width = math.gcd(total, 512)

    def look_advance(index, gathered):
        first = (index * width).astype(jnp.int32)
        block = lax.dynamic_slice_in_dim(table, first, width, 1)
        return gathered + jnp.dot(
            block,
            cell_hot(cells, first, width),
            precision=lax.Precision.HIGHEST,
            preferred_element_type=jnp.float32,
        )

    return lax.fori_loop(
        0, total // width, look_advance, jnp.zeros((table.shape[0], cells.shape[0]), jnp.float32)
    )


def deposit_into(source, cells, total):
    width = math.gcd(total, 512)

    def deposit_advance(index, field):
        first = (index * width).astype(jnp.int32)
        block = lax.dot_general(
            source,
            cell_hot(cells, first, width),
            (((1,), (1,)), ((), ())),
            precision=lax.Precision.HIGHEST,
            preferred_element_type=jnp.float32,
        )
        return lax.dynamic_update_slice_in_dim(field, block, first, 1)

    return lax.fori_loop(
        0, total // width, deposit_advance, jnp.zeros((source.shape[0], total), jnp.float32)
    )


def per_device(
    parcel_props, size_class, dest_owner, dest_local, class_table, gas_density, gas_rest
):
    width_x = lax.axis_size("gx")
    width_y = lax.axis_size("gy")
    devices = width_x * width_y
    parcels = parcel_props.shape[1]
    slab_x, slab_y = gas_density.shape
    capacity = max(2, 4 * parcels // devices)
    slots = devices * capacity
    owner = dest_owner[:, 0]
    member = (owner[:, None] == jnp.arange(devices, dtype=jnp.int32)[None, :]).astype(jnp.int32)
    rank = jnp.sum(jnp.cumsum(member, axis=0) * member, axis=1) - 1
    slot = owner * capacity + rank
    gas_flat = jnp.concatenate([gas_density[None], gas_rest], axis=0).reshape(5, slab_x * slab_y)
    float_buf = jnp.zeros((parcel_props.shape[0], slots), jnp.float32).at[:, slot].set(parcel_props)
    int_buf = (
        jnp.full((2, slots), -1, jnp.int32).at[:, slot].set(jnp.stack([size_class, dest_local]))
    )
    got_floats, got_ints = (
        lax.all_to_all(
            lax.all_to_all(
                float_buf.reshape(-1, width_x, width_y, capacity),
                "gx",
                split_axis=1,
                concat_axis=1,
                tiled=True,
            ),
            "gy",
            split_axis=2,
            concat_axis=2,
            tiled=True,
        ),
        lax.all_to_all(
            lax.all_to_all(
                int_buf.reshape(2, width_x, width_y, capacity),
                "gx",
                split_axis=1,
                concat_axis=1,
                tiled=True,
            ),
            "gy",
            split_axis=2,
            concat_axis=2,
            tiled=True,
        ),
    )
    props_in = got_floats.reshape(parcel_props.shape[0], slots)
    ints_in = got_ints.reshape(2, slots)
    cells = ints_in[1]
    safe = jnp.maximum(cells, 0)
    source = sources_of(props_in, ints_in[0], look_up(gas_flat, safe), class_table)
    deposit = deposit_into(source, cells, slab_x * slab_y).reshape(5, slab_x, slab_y)
    padded = with_halo(deposit, (("gx", 1), ("gy", 2)), 1)
    beside = padded[:, 2:, 1:-1] + padded[:, :-2, 1:-1] + padded[:, 1:-1, 2:] + padded[:, 1:-1, :-2]
    smooth = 0.4 * deposit + 0.15 * beside
    return (gas_density + smooth[0], gas_rest + smooth[1:])


def solution(mesh):
    return jax.shard_map(
        per_device,
        mesh=mesh,
        in_specs=(
            P(None, ("gx", "gy")),
            P(("gx", "gy")),
            P(("gx", "gy"), None),
            P(("gx", "gy")),
            P(),
            P("gx", "gy"),
            P(None, "gx", "gy"),
        ),
        out_specs=(P("gx", "gy"), P(None, "gx", "gy")),
        check_vma=False,
    )
```

profile of v0, /device:TPU:9, one launch (start us, length us, event | category | flops | bytes accessed | tf_op | source)
XLA Modules:
  0.0 324.7 jit_solution(1331157601480989141)
XLA Ops:
  1.4 9.2 %reduce-window.6 = s32[32,32,128]{2,1,0:T(8,128)S(1)} reduce-window(s32[32,32,128]{2,1,0:T(8,128)S(1)} %fusion.26, s32[]{:T(128)} %constant.78.clone.1), window={size=1x1x128 pad=0_0x0_0x127_0}, to_apply=%region_0.0 | reduce-window | flops 16646144 | bytes 1048580 | tf_op jit(solution)/shard_map/reduce-window
  15.1 14.3 %scatter_custom_fusion = s32[2,16384]{0,1:T(8,128)} fusion(s32[4096]{0:T(1024)S(1)} %bitcast.88, s32[4096,2]{1,0:T(8,128)S(1)} %copy.15, s32[]{:T(128)} %constant.80.clone.1), kind=kCustom, calls=%fused_computation.20 | custom fusion | bytes 131076 | tf_op jit(solution)/shard_map/scatter | solution.py:101
  34.6 9.9 %all_to_all.20 = s32[2,8,4,512]{3,2,0,1:T(4,128)S(1)} all-to-all(s32[2,8,4,512]{3,2,0,1:T(4,128)S(1)} %copy.16), channel_id=1, replica_groups=mesh['gx'=8,'gy'=4] {'gx'}, dimensions={1} | all-to-all | bytes 262144 | tf_op jit(solution)/shard_map/all_to_all | solution.py:118
  51.2 14.3 %scatter_custom_fusion.1 = f32[16,16384]{0,1:T(8,128)} fusion(s32[4096]{0:T(1024)S(1)} %bitcast.89, f32[4096,16]{1,0:T(8,128)S(1)} %copy.19, f32[]{:T(128)} %constant.79.clone.1), kind=kCustom, calls=%fused_computation.18 | custom fusion | bytes 1048580 | tf_op jit(solution)/shard_map/scatter | solution.py:99
  65.5 6.0 %copy.20 = f32[16,8,4,512]{3,2,0,1:T(4,128)} copy(f32[16,8,4,512]{0,3,2,1:T(8,128)} %bitcast.65) | data formatting | bytes 2097152 | tf_op jit(solution)/shard_map/reshape | solution.py:106
  77.2 23.9 %all-to-all-done.2 = f32[16,8,4,512]{3,2,0,1:T(4,128)S(1)} async-done(((f32[16,8,4,512]{3,2,0,1:T(4,128)}), f32[16,8,4,512]{3,2,0,1:T(4,128)S(1)}, u32[]{:S(2)}, u32[]{:S(2)}) %all-to-all-start.2) | async-done | bytes 1048608 | tf_op jit(solution)/shard_map/all_to_all | solution.py:105
  106.5 75.1 %while.28 = (s32[]{:T(128)}, f32[5,16384]{1,0:T(8,128)S(1)}, f32[5,4096]{1,0:T(8,128)S(1)}, s32[16384]{0:T(1024)S(1)}, s32[]{:T(128)}, /*index=5*/s32[]{:T(128)}, s32[]{:T(128)}, s32[]{:T(128)}) while((s32[]{:T(128)}, f32[5,16384]{1,0:T(8,128)S(1)}, f32[5,4096]{1,0:T(8,128)S(1)}, s32[16384]{0:T(1024)S(1)}, s32[]{:T(128)}, ...), condition=%wide.region_6.7_spmd.clone, body=%wide.region_5.6_spmd.clone.sunk | while | flops 511869440 | bytes 938141 | solution.py:60
  106.5 9.4 %fusion.54 = f32[5,16384]{1,0:T(8,128)S(1)} fusion(s32[16384]{0:T(1024)S(1)} %get-tuple-element.276, s32[512]{0:T(512)S(1)} %iota_add_fusion.5, f32[5,16384]{1,0:T(8,128)S(1)} %get-tuple-element.266, pred[]{:T(512)S(6)} %compare.3, f32[5,4096]{1,0:T(8,128)S(1)} %get-tuple-element.275, s32[]{:T(128)S(6)} %select_n.38), kind=kOutput, calls=%fused_computation.11.clone.1 | convolution fusion | flops 511868928 | bytes 935941 | tf_op jit(solution)/shard_map/while/body/eval_jaxpr/dot_general | solution.py:53
  115.9 9.4 %fusion.54 = f32[5,16384]{1,0:T(8,128)S(1)} fusion(s32[16384]{0:T(1024)S(1)} %get-tuple-element.276, s32[512]{0:T(512)S(1)} %iota_add_fusion.5, f32[5,16384]{1,0:T(8,128)S(1)} %get-tuple-element.266, pred[]{:T(512)S(6)} %compare.3, f32[5,4096]{1,0:T(8,128)S(1)} %get-tuple-element.275, s32[]{:T(128)S(6)} %select_n.38), kind=kOutput, calls=%fused_computation.11.clone.1 | convolution fusion | flops 511868928 | bytes 935941 | tf_op jit(solution)/shard_map/while/body/eval_jaxpr/dot_general | solution.py:53
  125.3 9.4 %fusion.54 = f32[5,16384]{1,0:T(8,128)S(1)} fusion(s32[16384]{0:T(1024)S(1)} %get-tuple-element.276, s32[512]{0:T(512)S(1)} %iota_add_fusion.5, f32[5,16384]{1,0:T(8,128)S(1)} %get-tuple-element.266, pred[]{:T(512)S(6)} %compare.3, f32[5,4096]{1,0:T(8,128)S(1)} %get-tuple-element.275, s32[]{:T(128)S(6)} %select_n.38), kind=kOutput, calls=%fused_computation.11.clone.1 | convolution fusion | flops 511868928 | bytes 935941 | tf_op jit(solution)/shard_map/while/body/eval_jaxpr/dot_general | solution.py:53
  134.7 9.4 %fusion.54 = f32[5,16384]{1,0:T(8,128)S(1)} fusion(s32[16384]{0:T(1024)S(1)} %get-tuple-element.276, s32[512]{0:T(512)S(1)} %iota_add_fusion.5, f32[5,16384]{1,0:T(8,128)S(1)} %get-tuple-element.266, pred[]{:T(512)S(6)} %compare.3, f32[5,4096]{1,0:T(8,128)S(1)} %get-tuple-element.275, s32[]{:T(128)S(6)} %select_n.38), kind=kOutput, calls=%fused_computation.11.clone.1 | convolution fusion | flops 511868928 | bytes 935941 | tf_op jit(solution)/shard_map/while/body/eval_jaxpr/dot_general | solution.py:53
  144.1 9.4 %fusion.54 = f32[5,16384]{1,0:T(8,128)S(1)} fusion(s32[16384]{0:T(1024)S(1)} %get-tuple-element.276, s32[512]{0:T(512)S(1)} %iota_add_fusion.5, f32[5,16384]{1,0:T(8,128)S(1)} %get-tuple-element.266, pred[]{:T(512)S(6)} %compare.3, f32[5,4096]{1,0:T(8,128)S(1)} %get-tuple-element.275, s32[]{:T(128)S(6)} %select_n.38), kind=kOutput, calls=%fused_computation.11.clone.1 | convolution fusion | flops 511868928 | bytes 935941 | tf_op jit(solution)/shard_map/while/body/eval_jaxpr/dot_general | solution.py:53
  153.5 9.4 %fusion.54 = f32[5,16384]{1,0:T(8,128)S(1)} fusion(s32[16384]{0:T(1024)S(1)} %get-tuple-element.276, s32[512]{0:T(512)S(1)} %iota_add_fusion.5, f32[5,16384]{1,0:T(8,128)S(1)} %get-tuple-element.266, pred[]{:T(512)S(6)} %compare.3, f32[5,4096]{1,0:T(8,128)S(1)} %get-tuple-element.275, s32[]{:T(128)S(6)} %select_n.38), kind=kOutput, calls=%fused_computation.11.clone.1 | convolution fusion | flops 511868928 | bytes 935941 | tf_op jit(solution)/shard_map/while/body/eval_jaxpr/dot_general | solution.py:53
  162.8 9.4 %fusion.54 = f32[5,16384]{1,0:T(8,128)S(1)} fusion(s32[16384]{0:T(1024)S(1)} %get-tuple-element.276, s32[512]{0:T(512)S(1)} %iota_add_fusion.5, f32[5,16384]{1,0:T(8,128)S(1)} %get-tuple-element.266, pred[]{:T(512)S(6)} %compare.3, f32[5,4096]{1,0:T(8,128)S(1)} %get-tuple-element.275, s32[]{:T(128)S(6)} %select_n.38), kind=kOutput, calls=%fused_computation.11.clone.1 | convolution fusion | flops 511868928 | bytes 935941 | tf_op jit(solution)/shard_map/while/body/eval_jaxpr/dot_general | solution.py:53
  172.2 9.4 %fusion.54 = f32[5,16384]{1,0:T(8,128)S(1)} fusion(s32[16384]{0:T(1024)S(1)} %get-tuple-element.276, s32[512]{0:T(512)S(1)} %iota_add_fusion.5, f32[5,16384]{1,0:T(8,128)S(1)} %get-tuple-element.266, pred[]{:T(512)S(6)} %compare.3, f32[5,4096]{1,0:T(8,128)S(1)} %get-tuple-element.275, s32[]{:T(128)S(6)} %select_n.38), kind=kOutput, calls=%fused_computation.11.clone.1 | convolution fusion | flops 511868928 | bytes 935941 | tf_op jit(solution)/shard_map/while/body/eval_jaxpr/dot_general | solution.py:53
  191.6 110.3 %while.27 = (s32[]{:T(128)}, f32[5,4096]{1,0:T(8,128)S(1)}, s32[1,16384]{1,0:T(1,128)S(1)}, f32[5,16384]{1,0:T(8,128)S(1)}, s32[]{:T(128)}, /*index=5*/s32[]{:T(128)}, s32[]{:T(128)}, s32[]{:T(128)}) while((s32[]{:T(128)}, f32[5,4096]{1,0:T(8,128)S(1)}, s32[1,16384]{1,0:T(1,128)S(1)}, f32[5,16384]{1,0:T(8,128)S(1)}, s32[]{:T(128)}, ...), condition=%wide.region_10.11_spmd, body=%wide.region_9.10_spmd.sunk | while | flops 511705600 | bytes 610451 | solution.py:79
  191.9 13.7 %fusion.51 = f32[5,4096]{1,0:T(8,128)S(1)} fusion(f32[5,4096]{1,0:T(8,128)S(1)} %get-tuple-element.290, s32[]{:T(128)S(6)} %select_n.37, f32[5,16384]{1,0:T(8,128)S(1)} %get-tuple-element.300, s32[16384]{0:T(1024)S(1)} %bitcast.85, s32[512]{0:T(512)S(1)} %iota_add_fusion.4), kind=kOutput, calls=%fused_computation.7.clone.1 | convolution fusion | flops 511705088 | bytes 608260 | tf_op jit(solution)/shard_map/while/body/eval_jaxpr/dot_general | solution.py:70
  205.6 13.8 %fusion.51 = f32[5,4096]{1,0:T(8,128)S(1)} fusion(f32[5,4096]{1,0:T(8,128)S(1)} %get-tuple-element.290, s32[]{:T(128)S(6)} %select_n.37, f32[5,16384]{1,0:T(8,128)S(1)} %get-tuple-element.300, s32[16384]{0:T(1024)S(1)} %bitcast.85, s32[512]{0:T(512)S(1)} %iota_add_fusion.4), kind=kOutput, calls=%fused_computation.7.clone.1 | convolution fusion | flops 511705088 | bytes 608260 | tf_op jit(solution)/shard_map/while/body/eval_jaxpr/dot_general | solution.py:70
  219.4 13.8 %fusion.51 = f32[5,4096]{1,0:T(8,128)S(1)} fusion(f32[5,4096]{1,0:T(8,128)S(1)} %get-tuple-element.290, s32[]{:T(128)S(6)} %select_n.37, f32[5,16384]{1,0:T(8,128)S(1)} %get-tuple-element.300, s32[16384]{0:T(1024)S(1)} %bitcast.85, s32[512]{0:T(512)S(1)} %iota_add_fusion.4), kind=kOutput, calls=%fused_computation.7.clone.1 | convolution fusion | flops 511705088 | bytes 608260 | tf_op jit(solution)/shard_map/while/body/eval_jaxpr/dot_general | solution.py:70
  233.2 13.8 %fusion.51 = f32[5,4096]{1,0:T(8,128)S(1)} fusion(f32[5,4096]{1,0:T(8,128)S(1)} %get-tuple-element.290, s32[]{:T(128)S(6)} %select_n.37, f32[5,16384]{1,0:T(8,128)S(1)} %get-tuple-element.300, s32[16384]{0:T(1024)S(1)} %bitcast.85, s32[512]{0:T(512)S(1)} %iota_add_fusion.4), kind=kOutput, calls=%fused_computation.7.clone.1 | convolution fusion | flops 511705088 | bytes 608260 | tf_op jit(solution)/shard_map/while/body/eval_jaxpr/dot_general | solution.py:70
  246.9 13.8 %fusion.51 = f32[5,4096]{1,0:T(8,128)S(1)} fusion(f32[5,4096]{1,0:T(8,128)S(1)} %get-tuple-element.290, s32[]{:T(128)S(6)} %select_n.37, f32[5,16384]{1,0:T(8,128)S(1)} %get-tuple-element.300, s32[16384]{0:T(1024)S(1)} %bitcast.85, s32[512]{0:T(512)S(1)} %iota_add_fusion.4), kind=kOutput, calls=%fused_computation.7.clone.1 | convolution fusion | flops 511705088 | bytes 608260 | tf_op jit(solution)/shard_map/while/body/eval_jaxpr/dot_general | solution.py:70
  260.7 13.8 %fusion.51 = f32[5,4096]{1,0:T(8,128)S(1)} fusion(f32[5,4096]{1,0:T(8,128)S(1)} %get-tuple-element.290, s32[]{:T(128)S(6)} %select_n.37, f32[5,16384]{1,0:T(8,128)S(1)} %get-tuple-element.300, s32[16384]{0:T(1024)S(1)} %bitcast.85, s32[512]{0:T(512)S(1)} %iota_add_fusion.4), kind=kOutput, calls=%fused_computation.7.clone.1 | convolution fusion | flops 511705088 | bytes 608260 | tf_op jit(solution)/shard_map/while/body/eval_jaxpr/dot_general | solution.py:70
  274.5 13.8 %fusion.51 = f32[5,4096]{1,0:T(8,128)S(1)} fusion(f32[5,4096]{1,0:T(8,128)S(1)} %get-tuple-element.290, s32[]{:T(128)S(6)} %select_n.37, f32[5,16384]{1,0:T(8,128)S(1)} %get-tuple-element.300, s32[16384]{0:T(1024)S(1)} %bitcast.85, s32[512]{0:T(512)S(1)} %iota_add_fusion.4), kind=kOutput, calls=%fused_computation.7.clone.1 | convolution fusion | flops 511705088 | bytes 608260 | tf_op jit(solution)/shard_map/while/body/eval_jaxpr/dot_general | solution.py:70
  288.2 13.8 %fusion.51 = f32[5,4096]{1,0:T(8,128)S(1)} fusion(f32[5,4096]{1,0:T(8,128)S(1)} %get-tuple-element.290, s32[]{:T(128)S(6)} %select_n.37, f32[5,16384]{1,0:T(8,128)S(1)} %get-tuple-element.300, s32[16384]{0:T(1024)S(1)} %bitcast.85, s32[512]{0:T(512)S(1)} %iota_add_fusion.4), kind=kOutput, calls=%fused_computation.7.clone.1 | convolution fusion | flops 511705088 | bytes 608260 | tf_op jit(solution)/shard_map/while/body/eval_jaxpr/dot_general | solution.py:70
  (90 shorter events, 60.7 us)
Async XLA Ops:
  0.6 181.8 %copy-start = (f32[8,16]{1,0:T(8,128)S(1)}, f32[8,16]{1,0:T(8,128)}, u32[]{:S(2)}) copy-start(f32[8,16]{1,0:T(8,128)} %param.15) | copy-start | bytes 1540
  15.1 35.5 %copy-start.2 = (f32[16,4096]{1,0:T(8,128)S(1)}, f32[16,4096]{1,0:T(8,128)}, u32[]{:S(2)}) copy-start(f32[16,4096]{1,0:T(8,128)} %param.11) | copy-start | bytes 786436
  45.3 26.3 %all-to-all-start.1 = ((s32[2,8,4,512]{3,1,0,2:T(8,128)}), s32[2,8,4,512]{3,1,0,2:T(8,128)S(1)}, u32[]{:S(2)}, u32[]{:S(2)}) async-start(s32[2,8,4,512]{3,1,0,2:T(8,128)} %copy.17), calls=%async_computation.1 | async-start | bytes 262144 | tf_op jit(solution)/shard_map/all_to_all | solution.py:117
  51.2 25.7 %copy-start.3 = (f32[4,32,128]{2,1,0:T(8,128)S(1)}, f32[4,32,128]{2,1,0:T(8,128)}, u32[]{:S(2)}) copy-start(f32[4,32,128]{2,1,0:T(8,128)} %param.17) | copy-start | bytes 196612
  51.2 25.8 %copy-start.4 = (f32[32,128]{1,0:T(8,128)S(1)}, f32[32,128]{1,0:T(8,128)}, u32[]{:S(2)}) copy-start(f32[32,128]{1,0:T(8,128)} %param.16) | copy-start | bytes 49156
  71.6 29.5 %all-to-all-start.2 = ((f32[16,8,4,512]{3,2,0,1:T(4,128)}), f32[16,8,4,512]{3,2,0,1:T(4,128)S(1)}, u32[]{:S(2)}, u32[]{:S(2)}) async-start(f32[16,8,4,512]{3,2,0,1:T(4,128)} %copy.20), calls=%async_computation.2 | async-start | bytes 2097152 | tf_op jit(solution)/shard_map/all_to_all | solution.py:105
  102.6 80.4 %all-to-all-start.3 = ((f32[16,8,4,512]{3,1,0,2:T(8,128)}), f32[16,8,4,512]{3,1,0,2:T(8,128)S(1)}, u32[]{:S(2)}, u32[]{:S(2)}) async-start(f32[16,8,4,512]{3,1,0,2:T(8,128)} %copy.21), calls=%async_computation.3 | async-start | bytes 2097152 | tf_op jit(solution)/shard_map/all_to_all | solution.py:104
  181.6 0.8 copy-start.1
  191.6 131.8 %copy-start.5 = (f32[32,128]{1,0:T(8,128)S(1)}, f32[32,128]{1,0:T(8,128)}, u32[]{:S(2)}) copy-start(f32[32,128]{1,0:T(8,128)} %param.16) | copy-start | bytes 49156
  302.0 6.9 %collective-permute-start = (f32[5,1,128]{2,1,0:T(1,128)S(1)}, f32[5,1,128]{2,1,0:T(1,128)S(1)}, u32[]{:S(2)}, u32[]{:S(2)}) collective-permute-start(f32[5,1,128]{2,1,0:T(1,128)S(1)} %get-tuple-element.204), channel_id=1, source_target_pairs={{4,0},{8,4},{12,8},{16,12},{20,16},{24,20},{28,24},{5,1},{9,5},{13... | collective-permute-start | bytes 7688 | tf_op jit(solution)/shard_map/ppermute | solution.py:16
  307.0 5.2 %collective-permute-start.1 = (f32[5,1,128]{2,1,0:T(1,128)S(1)}, f32[5,1,128]{2,1,0:T(1,128)S(1)}, u32[]{:S(2)}, u32[]{:S(2)}) collective-permute-start(f32[5,1,128]{2,1,0:T(1,128)S(1)} %get-tuple-element.203), channel_id=1, source_target_pairs={{0,4},{4,8},{8,12},{12,16},{16,20},{20,24},{24,28},{1,5},{5,9},{9,... | collective-permute-start | bytes 7688 | tf_op jit(solution)/shard_map/ppermute | solution.py:15
  312.3 6.9 %collective-permute-start.3 = (f32[5,34,1]{2,1,0:T(8,128)S(1)}, f32[5,34,1]{2,1,0:T(8,128)S(1)}, u32[]{:S(2)}, u32[]{:S(2)}) collective-permute-start(f32[5,34,1]{2,1,0:T(8,128)S(1)} %get-tuple-element.202), channel_id=1, source_target_pairs={{0,1},{1,2},{2,3},{4,5},{5,6},{6,7},{8,9},{9,10},{10,11},{12,13},{... | collective-permute-start | bytes 2048 | tf_op jit(solution)/shard_map/ppermute | solution.py:15
  317.3 6.0 %collective-permute-start.2 = (f32[5,34,1]{2,1,0:T(8,128)S(1)}, f32[5,34,1]{2,1,0:T(8,128)S(1)}, u32[]{:S(2)}, u32[]{:S(2)}) collective-permute-start(f32[5,34,1]{2,1,0:T(8,128)S(1)} %get-tuple-element.201), channel_id=1, source_target_pairs={{1,0},{2,1},{3,2},{5,4},{6,5},{7,6},{9,8},{10,9},{11,10},{13,12},{... | collective-permute-start | bytes 2048 | tf_op jit(solution)/shard_map/ppermute | solution.py:16
where the time goes:
time: 326 us; the launch traced here: 325 us
  matrix products  186 us (57%)
  local copies, waits for them, and re-layouts  48.9 us (15%)
  waiting for transfers between devices  31.2 us (10%)
  starting transfers between devices  28.3 us (9%)
  other arithmetic  19.4 us (6%)
  blocking collectives  9.88 us (3%)
    dot_general x8, matrix products, deposit_advance(): lax.dot_general(source, cell_hot(cells, first, width), (((1,), (1,)), (()...  110 us
    dot_general x8, matrix products, look_advance(): jnp.dot(block, cell_hot(cells, first, width), precision=lax.Precision.HIG...  75 us
    all_to_all x1, waiting for transfers between devices, per_device(): lax.all_to_all(float_buf.reshape(-1, width_x, width_y, capacity), 'gx', s...  23.9 us
    scatter x1, local copies, waits for them, and re-layouts, per_device(): jnp.full((2, slots), -1, jnp.int32).at[:, slot]  14.3 us
    scatter x1, local copies, waits for them, and re-layouts, per_device(): jnp.zeros((parcel_props.shape[0], slots), jnp.float32).at[:, slot]  14.3 us
    all_to_all x1, blocking collectives, per_device(): lax.all_to_all(int_buf.reshape(2, width_x, width_y, capacity), 'gx', spli...  9.88 us
    another operation x3, other arithmetic  9.62 us
    ppermute x2, starting transfers between devices, with_halo(): before = lax.ppermute(last, axis, up)  6.89 us
  transfers between devices with their start and end apart: 7, of which 3 were waited for; matrix products, arithmetic and copies ran while one was open for 30% of the time, Pallas kernels for 0%

commit v1 on v0

--- a/solution.py
+++ b/solution.py
@@ -102,12 +102,20 @@
     )
     got_floats, got_ints = (
         lax.all_to_all(
-            lax.all_to_all(
-                float_buf.reshape(-1, width_x, width_y, capacity),
-                "gx",
-                split_axis=1,
-                concat_axis=1,
-                tiled=True,
+            jnp.concatenate(
+                lax.all_to_all(
+                    jnp.stack(
+                        jnp.split(
+                            float_buf.reshape(-1, width_x, width_y, capacity),
+                            lax.axis_size("gx"),
+                            axis=1,
+                        )
+                    ),
+                    "gx",
+                    0,
+                    0,
+                ),
+                axis=1,
             ),
             "gy",
             split_axis=2,

time: 326 us -> 347 us (1.064)
  local copies, waits for them, and re-layouts: 48.9 us -> 68.1 us
  blocking collectives: 9.88 us -> 0 us
  starting transfers between devices: 28.3 us -> 34.8 us
  matrix products: 186 us -> 192 us
    unnamed x18 -> x31, local copies, waits for them, and re-layouts: 1.4 us -> 18 us
    all_to_all x1 -> x0, blocking collectives: 9.88 us -> none  [per_device(): lax.all_to_all(int_buf.reshape(2, width_x, width_y, capacity), 'gx', spli...]
    all_to_all x2 -> x3, starting transfers between devices: 9.27 us -> 16.6 us  [the longest x1 5.69 us: per_device(): lax.all_to_all(int_buf.reshape(2, width_x, width_y, capacity), 'gx', spli...]
    dot_general x8, matrix products: 110 us -> 117 us  [deposit_advance(): lax.dot_general(source, cell_hot(cells, first, width), (((1,), (1,)), (()...]
    split x0 -> x1, local copies, waits for them, and re-layouts: none -> 5.82 us  [per_device(): jnp.split(float_buf.reshape(-1, width_x, width_y, capacity), lax.axis_siz...]
    reshape x1, local copies, waits for them, and re-layouts: 6.02 us -> 1.58 us  [per_device(): jnp.concatenate(lax.all_to_all(jnp.stack(jnp.split(float_buf.reshape(-1,...]
    ppermute x2, waiting for transfers between devices: 4.04 us -> 0.4 us  [with_halo(): after = lax.ppermute(leading, axis, down)]
    all_to_all x2 -> x3, waiting for transfers between devices: 23.9 us -> 20.9 us  [the longest x1 20.8 us: per_device(): lax.all_to_all(jnp.stack(jnp.split(float_buf.reshape(-1, width_x, width_y...]
  transfers between devices with their start and end apart: 7 -> 8, of which waited for: 3 -> 5; matrix products, arithmetic and copies ran while one was open for 30% -> 34% of each run, Pallas kernels for 0% -> 0%
where the time goes in v1:
time: 347 us; the launch traced here: 345 us
  matrix products  192 us (55%)
  local copies, waits for them, and re-layouts  68.1 us (20%)
  starting transfers between devices  34.8 us (10%)
  waiting for transfers between devices  28.7 us (8%)
  other arithmetic  19.7 us (6%)
    dot_general x8, matrix products, deposit_advance(): lax.dot_general(source, cell_hot(cells, first, width), (((1,), (1,)), (()...  117 us
    dot_general x8, matrix products, look_advance(): jnp.dot(block, cell_hot(cells, first, width), precision=lax.Precision.HIG...  75 us
    all_to_all x1, waiting for transfers between devices, per_device(): lax.all_to_all(jnp.stack(jnp.split(float_buf.reshape(-1, width_x, width_y...  20.8 us
    unnamed x31, local copies, waits for them, and re-layouts  18 us
    scatter x1, local copies, waits for them, and re-layouts, per_device(): jnp.zeros((parcel_props.shape[0], slots), jnp.float32).at[:, slot]  14.3 us
    scatter x1, local copies, waits for them, and re-layouts, per_device(): jnp.full((2, slots), -1, jnp.int32).at[:, slot]  14.3 us
    another operation x3, other arithmetic  9.62 us
    ppermute x2, starting transfers between devices, with_halo(): after = lax.ppermute(leading, axis, down)  8.49 us
  transfers between devices with their start and end apart: 8, of which 5 were waited for; matrix products, arithmetic and copies ran while one was open for 34% of the time, Pallas kernels for 0%

profile of v1, /device:TPU:9, one launch (start us, length us, event | category | flops | bytes accessed | tf_op | source)
XLA Modules:
  0.0 344.9 jit_solution(5918385319247240529)
XLA Ops:
  1.4 9.2 %reduce-window.6 = s32[32,32,128]{2,1,0:T(8,128)S(1)} reduce-window(s32[32,32,128]{2,1,0:T(8,128)S(1)} %fusion.26, s32[]{:T(128)} %constant.78.clone.1), window={size=1x1x128 pad=0_0x0_0x127_0}, to_apply=%region_0.0 | reduce-window | flops 16646144 | bytes 1048580 | tf_op jit(solution)/shard_map/reduce-window
  15.1 14.3 %scatter_custom_fusion = s32[2,16384]{0,1:T(8,128)} fusion(s32[4096]{0:T(1024)S(1)} %bitcast.108, s32[4096,2]{1,0:T(8,128)S(1)} %copy.29, s32[]{:T(128)} %constant.80.clone.1), kind=kCustom, calls=%fused_computation.20 | custom fusion | bytes 131076 | tf_op jit(solution)/shard_map/scatter | solution.py:101
  29.4 5.8 %copy.30 = s32[2,8,4,512]{3,2,0,1:T(4,128)} copy(s32[2,8,4,512]{0,3,2,1:T(8,128)} %bitcast.84) | data formatting | bytes 262144 | tf_op jit(solution)/shard_map/reshape | solution.py:127
  41.6 14.3 %scatter_custom_fusion.1 = f32[16,16384]{0,1:T(8,128)} fusion(s32[4096]{0:T(1024)S(1)} %bitcast.109, f32[4096,16]{1,0:T(8,128)S(1)} %copy.33, f32[]{:T(128)} %constant.79.clone.1), kind=kCustom, calls=%fused_computation.18 | custom fusion | bytes 1048580 | tf_op jit(solution)/shard_map/scatter | solution.py:99
  55.9 5.8 %fusion.39 = (f32[16,1,4,512]{0,3,2,1:T(8,128)S(1)}, f32[16,1,4,512]{0,3,2,1:T(8,128)S(1)}, f32[16,1,4,512]{0,3,2,1:T(8,128)S(1)}, f32[16,1,4,512]{0,3,2,1:T(8,1...) fusion(f32[16,8,4,512]{0,3,2,1:T(8,128)} %bitcast.83), kind=kLoop, calls=%fused_computation.84 | loop fusion | bytes 2097152 | tf_op jit(solution)/shard_map/split | solution.py:108
  95.0 20.8 %all-to-all-done.2 = f32[8,16,1,4,512]{4,3,1,2,0:T(4,128)S(1)} async-done(((f32[8,16,1,4,512]{4,3,1,2,0:T(4,128)}), f32[8,16,1,4,512]{4,3,1,2,0:T(4,128)S(1)}, u32[]{:S(2)}, u32[]{:S(2)}) %all-to-all-start.2) | async-done | bytes 1048608 | tf_op jit(solution)/shard_map/all_to_all | solution.py:106
  122.9 75.1 %while.28 = (s32[]{:T(128)}, f32[5,16384]{1,0:T(8,128)S(1)}, f32[5,4096]{1,0:T(8,128)S(1)}, s32[16384]{0:T(1024)S(1)}, s32[]{:T(128)}, /*index=5*/s32[]{:T(128)}, s32[]{:T(128)}, s32[]{:T(128)}) while((s32[]{:T(128)}, f32[5,16384]{1,0:T(8,128)S(1)}, f32[5,4096]{1,0:T(8,128)S(1)}, s32[16384]{0:T(1024)S(1)}, s32[]{:T(128)}, ...), condition=%wide.region_6.7_spmd.clone, body=%wide.region_5.6_spmd.clone.sunk | while | flops 511869440 | bytes 938133 | solution.py:60
  122.9 9.4 %fusion.55 = f32[5,16384]{1,0:T(8,128)S(1)} fusion(s32[16384]{0:T(1024)S(1)} %get-tuple-element.284, s32[512]{0:T(512)S(1)} %iota_add_fusion.5, f32[5,16384]{1,0:T(8,128)S(1)} %get-tuple-element.274, pred[]{:T(512)S(6)} %compare.3, f32[5,4096]{1,0:T(8,128)S(1)} %get-tuple-element.283, s32[]{:T(128)S(6)} %select_n.38), kind=kOutput, calls=%fused_computation.11.clone.1 | convolution fusion | flops 511868928 | bytes 935941 | tf_op jit(solution)/shard_map/while/body/eval_jaxpr/dot_general | solution.py:53
  132.3 9.4 %fusion.55 = f32[5,16384]{1,0:T(8,128)S(1)} fusion(s32[16384]{0:T(1024)S(1)} %get-tuple-element.284, s32[512]{0:T(512)S(1)} %iota_add_fusion.5, f32[5,16384]{1,0:T(8,128)S(1)} %get-tuple-element.274, pred[]{:T(512)S(6)} %compare.3, f32[5,4096]{1,0:T(8,128)S(1)} %get-tuple-element.283, s32[]{:T(128)S(6)} %select_n.38), kind=kOutput, calls=%fused_computation.11.clone.1 | convolution fusion | flops 511868928 | bytes 935941 | tf_op jit(solution)/shard_map/while/body/eval_jaxpr/dot_general | solution.py:53
  141.7 9.4 %fusion.55 = f32[5,16384]{1,0:T(8,128)S(1)} fusion(s32[16384]{0:T(1024)S(1)} %get-tuple-element.284, s32[512]{0:T(512)S(1)} %iota_add_fusion.5, f32[5,16384]{1,0:T(8,128)S(1)} %get-tuple-element.274, pred[]{:T(512)S(6)} %compare.3, f32[5,4096]{1,0:T(8,128)S(1)} %get-tuple-element.283, s32[]{:T(128)S(6)} %select_n.38), kind=kOutput, calls=%fused_computation.11.clone.1 | convolution fusion | flops 511868928 | bytes 935941 | tf_op jit(solution)/shard_map/while/body/eval_jaxpr/dot_general | solution.py:53
  151.1 9.4 %fusion.55 = f32[5,16384]{1,0:T(8,128)S(1)} fusion(s32[16384]{0:T(1024)S(1)} %get-tuple-element.284, s32[512]{0:T(512)S(1)} %iota_add_fusion.5, f32[5,16384]{1,0:T(8,128)S(1)} %get-tuple-element.274, pred[]{:T(512)S(6)} %compare.3, f32[5,4096]{1,0:T(8,128)S(1)} %get-tuple-element.283, s32[]{:T(128)S(6)} %select_n.38), kind=kOutput, calls=%fused_computation.11.clone.1 | convolution fusion | flops 511868928 | bytes 935941 | tf_op jit(solution)/shard_map/while/body/eval_jaxpr/dot_general | solution.py:53
  160.4 9.4 %fusion.55 = f32[5,16384]{1,0:T(8,128)S(1)} fusion(s32[16384]{0:T(1024)S(1)} %get-tuple-element.284, s32[512]{0:T(512)S(1)} %iota_add_fusion.5, f32[5,16384]{1,0:T(8,128)S(1)} %get-tuple-element.274, pred[]{:T(512)S(6)} %compare.3, f32[5,4096]{1,0:T(8,128)S(1)} %get-tuple-element.283, s32[]{:T(128)S(6)} %select_n.38), kind=kOutput, calls=%fused_computation.11.clone.1 | convolution fusion | flops 511868928 | bytes 935941 | tf_op jit(solution)/shard_map/while/body/eval_jaxpr/dot_general | solution.py:53
  169.8 9.4 %fusion.55 = f32[5,16384]{1,0:T(8,128)S(1)} fusion(s32[16384]{0:T(1024)S(1)} %get-tuple-element.284, s32[512]{0:T(512)S(1)} %iota_add_fusion.5, f32[5,16384]{1,0:T(8,128)S(1)} %get-tuple-element.274, pred[]{:T(512)S(6)} %compare.3, f32[5,4096]{1,0:T(8,128)S(1)} %get-tuple-element.283, s32[]{:T(128)S(6)} %select_n.38), kind=kOutput, calls=%fused_computation.11.clone.1 | convolution fusion | flops 511868928 | bytes 935941 | tf_op jit(solution)/shard_map/while/body/eval_jaxpr/dot_general | solution.py:53
  179.2 9.4 %fusion.55 = f32[5,16384]{1,0:T(8,128)S(1)} fusion(s32[16384]{0:T(1024)S(1)} %get-tuple-element.284, s32[512]{0:T(512)S(1)} %iota_add_fusion.5, f32[5,16384]{1,0:T(8,128)S(1)} %get-tuple-element.274, pred[]{:T(512)S(6)} %compare.3, f32[5,4096]{1,0:T(8,128)S(1)} %get-tuple-element.283, s32[]{:T(128)S(6)} %select_n.38), kind=kOutput, calls=%fused_computation.11.clone.1 | convolution fusion | flops 511868928 | bytes 935941 | tf_op jit(solution)/shard_map/while/body/eval_jaxpr/dot_general | solution.py:53
  188.6 9.4 %fusion.55 = f32[5,16384]{1,0:T(8,128)S(1)} fusion(s32[16384]{0:T(1024)S(1)} %get-tuple-element.284, s32[512]{0:T(512)S(1)} %iota_add_fusion.5, f32[5,16384]{1,0:T(8,128)S(1)} %get-tuple-element.274, pred[]{:T(512)S(6)} %compare.3, f32[5,4096]{1,0:T(8,128)S(1)} %get-tuple-element.283, s32[]{:T(128)S(6)} %select_n.38), kind=kOutput, calls=%fused_computation.11.clone.1 | convolution fusion | flops 511868928 | bytes 935941 | tf_op jit(solution)/shard_map/while/body/eval_jaxpr/dot_general | solution.py:53
  207.7 116.9 %while.27 = (s32[]{:T(128)}, f32[5,4096]{1,0:T(8,128)S(1)}, s32[1,16384]{1,0:T(1,128)}, f32[5,16384]{1,0:T(8,128)S(1)}, s32[]{:T(128)}, /*index=5*/s32[]{:T(128)}, s32[]{:T(128)}, s32[]{:T(128)}) while((s32[]{:T(128)}, f32[5,4096]{1,0:T(8,128)S(1)}, s32[1,16384]{1,0:T(1,128)}, f32[5,16384]{1,0:T(8,128)S(1)}, s32[]{:T(128)}, ...), condition=%wide.region_10.11_spmd, body=%wide.region_9.10_spmd.sunk | while | flops 511705600 | bytes 610443 | solution.py:79
  207.9 14.6 %fusion.52 = f32[5,4096]{1,0:T(8,128)S(1)} fusion(f32[5,4096]{1,0:T(8,128)S(1)} %get-tuple-element.298, s32[]{:T(128)S(6)} %select_n.37, f32[5,16384]{1,0:T(8,128)S(1)} %get-tuple-element.308, s32[16384]{0:T(1024)} %bitcast.105, s32[512]{0:T(512)S(1)} %iota_add_fusion.4), kind=kOutput, calls=%fused_computation.7.clone.1 | convolution fusion | flops 511705088 | bytes 608260 | tf_op jit(solution)/shard_map/while/body/eval_jaxpr/dot_general | solution.py:70
  222.5 14.6 %fusion.52 = f32[5,4096]{1,0:T(8,128)S(1)} fusion(f32[5,4096]{1,0:T(8,128)S(1)} %get-tuple-element.298, s32[]{:T(128)S(6)} %select_n.37, f32[5,16384]{1,0:T(8,128)S(1)} %get-tuple-element.308, s32[16384]{0:T(1024)} %bitcast.105, s32[512]{0:T(512)S(1)} %iota_add_fusion.4), kind=kOutput, calls=%fused_computation.7.clone.1 | convolution fusion | flops 511705088 | bytes 608260 | tf_op jit(solution)/shard_map/while/body/eval_jaxpr/dot_general | solution.py:70
  237.1 14.6 %fusion.52 = f32[5,4096]{1,0:T(8,128)S(1)} fusion(f32[5,4096]{1,0:T(8,128)S(1)} %get-tuple-element.298, s32[]{:T(128)S(6)} %select_n.37, f32[5,16384]{1,0:T(8,128)S(1)} %get-tuple-element.308, s32[16384]{0:T(1024)} %bitcast.105, s32[512]{0:T(512)S(1)} %iota_add_fusion.4), kind=kOutput, calls=%fused_computation.7.clone.1 | convolution fusion | flops 511705088 | bytes 608260 | tf_op jit(solution)/shard_map/while/body/eval_jaxpr/dot_general | solution.py:70
  251.7 14.6 %fusion.52 = f32[5,4096]{1,0:T(8,128)S(1)} fusion(f32[5,4096]{1,0:T(8,128)S(1)} %get-tuple-element.298, s32[]{:T(128)S(6)} %select_n.37, f32[5,16384]{1,0:T(8,128)S(1)} %get-tuple-element.308, s32[16384]{0:T(1024)} %bitcast.105, s32[512]{0:T(512)S(1)} %iota_add_fusion.4), kind=kOutput, calls=%fused_computation.7.clone.1 | convolution fusion | flops 511705088 | bytes 608260 | tf_op jit(solution)/shard_map/while/body/eval_jaxpr/dot_general | solution.py:70
  266.3 14.6 %fusion.52 = f32[5,4096]{1,0:T(8,128)S(1)} fusion(f32[5,4096]{1,0:T(8,128)S(1)} %get-tuple-element.298, s32[]{:T(128)S(6)} %select_n.37, f32[5,16384]{1,0:T(8,128)S(1)} %get-tuple-element.308, s32[16384]{0:T(1024)} %bitcast.105, s32[512]{0:T(512)S(1)} %iota_add_fusion.4), kind=kOutput, calls=%fused_computation.7.clone.1 | convolution fusion | flops 511705088 | bytes 608260 | tf_op jit(solution)/shard_map/while/body/eval_jaxpr/dot_general | solution.py:70
  280.8 14.6 %fusion.52 = f32[5,4096]{1,0:T(8,128)S(1)} fusion(f32[5,4096]{1,0:T(8,128)S(1)} %get-tuple-element.298, s32[]{:T(128)S(6)} %select_n.37, f32[5,16384]{1,0:T(8,128)S(1)} %get-tuple-element.308, s32[16384]{0:T(1024)} %bitcast.105, s32[512]{0:T(512)S(1)} %iota_add_fusion.4), kind=kOutput, calls=%fused_computation.7.clone.1 | convolution fusion | flops 511705088 | bytes 608260 | tf_op jit(solution)/shard_map/while/body/eval_jaxpr/dot_general | solution.py:70
  295.4 14.6 %fusion.52 = f32[5,4096]{1,0:T(8,128)S(1)} fusion(f32[5,4096]{1,0:T(8,128)S(1)} %get-tuple-element.298, s32[]{:T(128)S(6)} %select_n.37, f32[5,16384]{1,0:T(8,128)S(1)} %get-tuple-element.308, s32[16384]{0:T(1024)} %bitcast.105, s32[512]{0:T(512)S(1)} %iota_add_fusion.4), kind=kOutput, calls=%fused_computation.7.clone.1 | convolution fusion | flops 511705088 | bytes 608260 | tf_op jit(solution)/shard_map/while/body/eval_jaxpr/dot_general | solution.py:70
  310.0 14.6 %fusion.52 = f32[5,4096]{1,0:T(8,128)S(1)} fusion(f32[5,4096]{1,0:T(8,128)S(1)} %get-tuple-element.298, s32[]{:T(128)S(6)} %select_n.37, f32[5,16384]{1,0:T(8,128)S(1)} %get-tuple-element.308, s32[16384]{0:T(1024)} %bitcast.105, s32[512]{0:T(512)S(1)} %iota_add_fusion.4), kind=kOutput, calls=%fused_computation.7.clone.1 | convolution fusion | flops 511705088 | bytes 608260 | tf_op jit(solution)/shard_map/while/body/eval_jaxpr/dot_general | solution.py:70
  (105 shorter events, 81.6 us)
Async XLA Ops:
  0.6 198.2 %copy-start = (f32[8,16]{1,0:T(8,128)S(1)}, f32[8,16]{1,0:T(8,128)}, u32[]{:S(2)}) copy-start(f32[8,16]{1,0:T(8,128)} %param.15) | copy-start | bytes 1540
  15.1 25.9 %copy-start.2 = (f32[16,4096]{1,0:T(8,128)S(1)}, f32[16,4096]{1,0:T(8,128)}, u32[]{:S(2)}) copy-start(f32[16,4096]{1,0:T(8,128)} %param.11) | copy-start | bytes 786436
  35.3 42.8 %all-to-all-start = ((s32[2,8,4,512]{3,2,0,1:T(4,128)}), s32[2,8,4,512]{3,2,0,1:T(4,128)}, u32[]{:S(2)}, u32[]{:S(2)}) async-start(s32[2,8,4,512]{3,2,0,1:T(4,128)} %copy.30), calls=%async_computation | async-start | bytes 262144 | tf_op jit(solution)/shard_map/all_to_all | solution.py:126
  79.7 8.1 %all-to-all-start.1 = ((s32[2,8,4,512]{3,1,0,2:T(8,128)}), s32[2,8,4,512]{3,1,0,2:T(8,128)S(1)}, u32[]{:S(2)}, u32[]{:S(2)}) async-start(s32[2,8,4,512]{3,1,0,2:T(8,128)} %copy.31), calls=%async_computation.1 | async-start | bytes 262144 | tf_op jit(solution)/shard_map/all_to_all | solution.py:125
  87.8 28.1 %all-to-all-start.2 = ((f32[8,16,1,4,512]{4,3,1,2,0:T(4,128)}), f32[8,16,1,4,512]{4,3,1,2,0:T(4,128)S(1)}, u32[]{:S(2)}, u32[]{:S(2)}) async-start(f32[8,16,1,4,512]{4,3,1,2,0:T(4,128)} %bitcast_dynamic-update-slice_fusion), calls=%async_computation.2 | async-start | bytes 2097152 | tf_op jit(solution)/shard_map/all_to_all | solution.py:106
  117.5 82.0 %all-to-all-start.3 = ((f32[16,8,4,512]{3,1,0,2:T(8,128)}), f32[16,8,4,512]{3,1,0,2:T(8,128)S(1)}, u32[]{:S(2)}, u32[]{:S(2)}) async-start(f32[16,8,4,512]{3,1,0,2:T(8,128)} %copy.42), calls=%async_computation.3 | async-start | bytes 2097152 | tf_op jit(solution)/shard_map/all_to_all | solution.py:104
  198.0 2.8 copy-start.1
  207.6 136.0 %copy-start.3 = (f32[4,32,128]{2,1,0:T(8,128)S(1)}, f32[4,32,128]{2,1,0:T(8,128)}, u32[]{:S(2)}) copy-start(f32[4,32,128]{2,1,0:T(8,128)} %param.17) | copy-start | bytes 196612
  207.6 136.6 %copy-start.4 = (f32[32,128]{1,0:T(8,128)S(1)}, f32[32,128]{1,0:T(8,128)}, u32[]{:S(2)}) copy-start(f32[32,128]{1,0:T(8,128)} %param.16) | copy-start | bytes 49156
  324.7 6.8 %collective-permute-start = (f32[5,1,128]{2,1,0:T(1,128)S(1)}, f32[5,1,128]{2,1,0:T(1,128)S(1)}, u32[]{:S(2)}, u32[]{:S(2)}) collective-permute-start(f32[5,1,128]{2,1,0:T(1,128)S(1)} %get-tuple-element.212), channel_id=1, source_target_pairs={{4,0},{8,4},{12,8},{16,12},{20,16},{24,20},{28,24},{5,1},{9,5},{13... | collective-permute-start | bytes 7688 | tf_op jit(solution)/shard_map/ppermute | solution.py:16
  329.6 5.2 %collective-permute-start.1 = (f32[5,1,128]{2,1,0:T(1,128)S(1)}, f32[5,1,128]{2,1,0:T(1,128)S(1)}, u32[]{:S(2)}, u32[]{:S(2)}) collective-permute-start(f32[5,1,128]{2,1,0:T(1,128)S(1)} %get-tuple-element.211), channel_id=1, source_target_pairs={{0,4},{4,8},{8,12},{12,16},{16,20},{20,24},{24,28},{1,5},{5,9},{9,... | collective-permute-start | bytes 7688 | tf_op jit(solution)/shard_map/ppermute | solution.py:15
  334.9 7.3 %collective-permute-start.2 = (f32[5,34,1]{2,1,0:T(8,128)S(1)}, f32[5,34,1]{2,1,0:T(8,128)S(1)}, u32[]{:S(2)}, u32[]{:S(2)}) collective-permute-start(f32[5,34,1]{2,1,0:T(8,128)S(1)} %get-tuple-element.209), channel_id=1, source_target_pairs={{1,0},{2,1},{3,2},{5,4},{6,5},{7,6},{9,8},{10,9},{11,10},{13,12},{... | collective-permute-start | bytes 2048 | tf_op jit(solution)/shard_map/ppermute | solution.py:16
  338.5 5.0 %collective-permute-start.3 = (f32[5,34,1]{2,1,0:T(8,128)S(1)}, f32[5,34,1]{2,1,0:T(8,128)S(1)}, u32[]{:S(2)}, u32[]{:S(2)}) collective-permute-start(f32[5,34,1]{2,1,0:T(8,128)S(1)} %get-tuple-element.210), channel_id=1, source_target_pairs={{0,1},{1,2},{2,3},{4,5},{5,6},{6,7},{8,9},{9,10},{10,11},{12,13},{... | collective-permute-start | bytes 2048 | tf_op jit(solution)/shard_map/ppermute | solution.py:15
